TPU v7x, 32 devices: a whole 2x2x4 slice. The times are simulated.
32 devices in a mesh: frame: 16 (over z, y, x), row: 2 (over core).
Axes of the slice: x: 2, y: 2, z: 4, core: 2. Of those that a mesh axis runs over, the one named last changes fastest.
Arguments:
- footage: float32 [64, 1024, 1024], P('frame', 'row'), may hold values from -30 to 30
Outputs:
- coefficients: float32 [64, 1024, 1024], P('frame', 'row')
- energies: float32 [4, 10], replicated
All inputs are finite; a program needn't handle non-finite values.
Results may differ from a plain program's by a relative error of at most 0.00007.
Values sent between devices are 32-bit elements; how exact they have to be, the bound alone decides.
A program may use at most 128 MiB of HBM per device.

v0:
```python
import jax
import jax.numpy as jnp
import numpy as np
from jax import lax
from jax.sharding import PartitionSpec as P

SLEVELS = 3
TLEVELS = 3


LIFT_ALPHA = -1.586134342
LIFT_BETA = -0.05298011854
LIFT_GAMMA = 0.8829110762
LIFT_DELTA = 0.4435068522
LIFT_ZETA = 1.149604398


def shifted(block, axis, distance):
    devices = range(lax.axis_size(axis))
    route = [(i - distance, i) for i in devices if i - distance in devices]
    return lax.ppermute(block, axis, route)


def mirror_after(values, along):
    length = values.shape[along]
    return jnp.concatenate(
        [
            lax.slice_in_dim(values, 1, length, axis=along),
            lax.slice_in_dim(values, length - 1, length, axis=along),
        ],
        axis=along,
    )


def mirror_before(values, along):
    length = values.shape[along]
    return jnp.concatenate(
        [
            lax.slice_in_dim(values, 0, 1, axis=along),
            lax.slice_in_dim(values, 0, length - 1, axis=along),
        ],
        axis=along,
    )


def weave_axis(even_part, odd_part, along):
    stacked = jnp.stack([even_part, odd_part], axis=along + 1)
    new_shape = list(even_part.shape)
    new_shape[along] = new_shape[along] * 2
    return stacked.reshape(tuple(new_shape))


def lift_pair(even_part, odd_part, take_next, take_prev):
    odd_part = odd_part + LIFT_ALPHA * (even_part + take_next(even_part))
    even_part = even_part + LIFT_BETA * (take_prev(odd_part) + odd_part)
    odd_part = odd_part + LIFT_GAMMA * (even_part + take_next(even_part))
    even_part = even_part + LIFT_DELTA * (take_prev(odd_part) + odd_part)
    return (even_part * LIFT_ZETA, odd_part * (1.0 / LIFT_ZETA))


def table_next(values):
    return np.concatenate([values[:, 1:], values[:, -1:]], axis=1)


def table_prev(values):
    return np.concatenate([values[:, :1], values[:, :-1]], axis=1)


def column_matrix(width):
    identity = np.eye(width)
    even_part = identity[:, 0::2]
    odd_part = identity[:, 1::2]
    odd_part = odd_part + LIFT_ALPHA * (even_part + table_next(even_part))
    even_part = even_part + LIFT_BETA * (table_prev(odd_part) + odd_part)
    odd_part = odd_part + LIFT_GAMMA * (even_part + table_next(even_part))
    even_part = even_part + LIFT_DELTA * (table_prev(odd_part) + odd_part)
    lifted = np.concatenate([even_part * LIFT_ZETA, odd_part * (1.0 / LIFT_ZETA)], axis=1)
    return jnp.asarray(lifted.astype(np.float32))


def spatial_inplace(block, levels):
    frame_count, row_count, width = block.shape
    mixed = jnp.dot(block, column_matrix(width), precision=lax.Precision.HIGHEST)
    paired = mixed.reshape(frame_count, row_count // 2, 2, width)
    low_rows, high_rows = lift_pair(paired[:, :, 0, :], paired[:, :, 1, :], rows_next, rows_prev)
    half_width = width // 2
    coarse = low_rows[..., :half_width]
    if levels > 1:
        coarse = spatial_inplace(coarse, levels - 1)
    upper_rows = weave_axis(coarse, low_rows[..., half_width:], 2)
    bottom = weave_axis(high_rows[..., :half_width], high_rows[..., half_width:], 2)
    return jnp.stack([upper_rows, bottom], axis=2).reshape(frame_count, row_count, width)


def temporal(planes_in, levels):
    even_part = planes_in[0::2]
    odd_part = planes_in[1::2]
    odd_part = odd_part - 0.5 * (even_part + mirror_after(even_part, 0))
    even_part = even_part + 0.25 * (mirror_before(odd_part, 0) + odd_part)
    if levels > 1:
        even_part = temporal(even_part, levels - 1)
    return weave_axis(even_part, odd_part, 0)


def rows_next(values):
    arrived = shifted(values[:, :1], "row", -1)
    is_last = lax.axis_index("row") == lax.axis_size("row") - 1
    return jnp.concatenate([values[:, 1:], jnp.where(is_last, values[:, -1:], arrived)], axis=1)


def rows_prev(values):
    arrived = shifted(values[:, -1:], "row", 1)
    is_first = lax.axis_index("row") == 0
    return jnp.concatenate([jnp.where(is_first, values[:, :1], arrived), values[:, :-1]], axis=1)


def level_of(number, ceiling):
    depth_now = 1
    while number % 2 == 0 and depth_now <= ceiling:
        number = number // 2
        depth_now = depth_now + 1
    return depth_now


def space_table(levels):
    period = 2**levels
    band_table = np.zeros((period * period, 3 * levels + 1), np.float32)
    for row_pos in range(period):
        for col_pos in range(period):
            row_level = level_of(row_pos, levels)
            col_level = level_of(col_pos, levels)
            finest = min(row_level, col_level)
            if finest > levels:
                column = 3 * levels
            elif row_level == col_level:
                column = 3 * (finest - 1) + 2
            elif row_level == finest:
                column = 3 * (finest - 1)
            else:
                column = 3 * (finest - 1) + 1
            band_table[row_pos * period + col_pos, column] = 1.0
    return band_table


def time_table(levels):
    period = 2**levels
    band_table = np.zeros((period, levels + 1), np.float32)
    for number in range(period):
        band_table[number, level_of(number, levels) - 1] = 1.0
    return band_table


def band_sums(coeffs, first_frame, levels_s, levels_t):
    period = 2**levels_s
    frame_count, row_count, col_count = coeffs.shape
    square = coeffs * coeffs
    row_folded = square.reshape(frame_count, row_count // period, period, col_count).sum(axis=1)
    column_phase = np.arange(col_count) % period
    selector = jnp.asarray((column_phase[:, None] == np.arange(period)[None, :]).astype(np.float32))
    pattern = jnp.dot(row_folded, selector, precision=lax.Precision.HIGHEST)
    pattern = pattern.reshape(frame_count, period * period)
    per_frame = jnp.dot(
        pattern, jnp.asarray(space_table(levels_s), jnp.float32), precision=lax.Precision.HIGHEST
    )
    time_period = 2**levels_t
    position = (first_frame + jnp.arange(frame_count, dtype=jnp.int32)) % time_period
    onehot = (position[:, None] == jnp.arange(time_period, dtype=jnp.int32)[None, :]).astype(
        jnp.float32
    )
    frame_band = jnp.dot(
        onehot, jnp.asarray(time_table(levels_t), jnp.float32), precision=lax.Precision.HIGHEST
    )
    return jnp.dot(frame_band.T, per_frame, precision=lax.Precision.HIGHEST)


def band_means(totals, frames_all, rows_all, cols_all, levels_s, levels_t):
    space_share = space_table(levels_s).sum(0) / float((2**levels_s) ** 2)
    time_share = time_table(levels_t).sum(0) / float(2**levels_t)
    counts = (
        float(frames_all) * float(rows_all) * float(cols_all) * np.outer(time_share, space_share)
    )
    return totals / jnp.asarray(counts, jnp.float32)


def shards(footage):
    frames_dev = footage.shape[0]
    planes = spatial_inplace(footage, SLEVELS)
    temporal_out = temporal(
        lax.all_to_all(planes, "frame", split_axis=1, concat_axis=0, tiled=True), TLEVELS
    )
    coeffs = lax.all_to_all(temporal_out, "frame", split_axis=0, concat_axis=1, tiled=True)
    totals = band_sums(coeffs, lax.axis_index("frame") * frames_dev, SLEVELS, TLEVELS)
    totals = lax.psum(totals, ("frame", "row"))
    means = band_means(
        totals,
        frames_dev * lax.axis_size("frame"),
        coeffs.shape[1] * lax.axis_size("row"),
        coeffs.shape[2],
        SLEVELS,
        TLEVELS,
    )
    return (coeffs, means)


def solution(mesh):
    return jax.shard_map(
        shards,
        mesh=mesh,
        in_specs=(P("frame", "row", None),),
        out_specs=(P("frame", "row", None), P()),
        check_vma=False,
    )
```

profile of v0, /device:TPU:0, one launch (start us, length us, event | category | flops | bytes accessed | tf_op | source)
XLA Modules:
  0.0 669.5 jit_solution(6688530232217569210)
XLA Ops:
  0.6 31.4 %convolution_bitcast_fusion = f32[4,512,1024]{2,1,0:T(8,128)} fusion(f32[1024,1024,1]{1,0,2:T(8,128)} %constant.85, f32[4,512,1024]{2,1,0:T(8,128)} %param.8), kind=kOutput, calls=%fused_computation.26 | convolution fusion | flops 25769803776 | bytes 20971520 | tf_op jit(solution)/shard_map/dot_general | solution.py:83
  32.0 10.6 %reshape.40 = f32[4,256,2,1024]{3,2,1,0:T(2,128)} reshape(f32[4,512,1024]{2,1,0:T(8,128)} %convolution_bitcast_fusion) | data formatting | bytes 16777216 | tf_op jit(solution)/shard_map/reshape | solution.py:84
  42.6 10.7 %fusion.50 = (f32[4,256,1,1024]{3,2,1,0:T(1,128)}, f32[4,256,1,1024]{3,2,1,0:T(1,128)S(1)}) fusion(f32[4,256,2,1024]{3,2,1,0:T(2,128)} %reshape.40), kind=kLoop, calls=%fused_computation.109 | loop fusion | bytes 16777216 | tf_op jit(solution)/shard_map/slice | solution.py:85
  57.4 2.5 slice.290
  60.8 7.3 %fusion.1 = f32[4,256,1024]{2,1,0:T(8,128)S(1)} fusion(f32[4,1,1024]{2,1,0:T(1,128)S(1)} %broadcast_select_fusion.1, f32[4,255,1024]{2,1,0:T(8,128)} %slice.290, f32[4,256,1,1024]{3,2,1,0:T(1,128)} %get-tuple-element.8, f32[4,256,1,1024]{3,2,1,0:T(1,128)} %copy-done.2), kind=kLoop, calls=%fused_computation.4 | loop fusion | flops 4194304 | bytes 16777216 | tf_op jit(solution)/shard_map/add | solution.py:54
  70.2 2.7 collective-permute-start.1
  74.4 6.8 %fusion.3 = f32[4,256,1024]{2,1,0:T(8,128)S(1)} fusion(f32[4,256,1024]{2,1,0:T(8,128)} %copy-done, f32[4,255,1024]{2,1,0:T(8,128)} %bitcast.99, f32[4,1,1024]{2,1,0:T(1,128)S(1)} %broadcast_select_fusion.3, f32[4,256,1,1024]{3,2,1,0:T(1,128)} %copy-done.2), kind=kLoop, calls=%fused_computation.7 | loop fusion | flops 4194304 | bytes 16777216 | tf_op jit(solution)/shard_map/add | solution.py:55
  82.8 2.5 slice.296
  85.3 5.8 broadcast_multiply_fusion
  91.1 3.0 collective-permute-start.3
  98.6 4.8 fusion.13
  103.4 2.5 reshape.41
  116.0 2.5 pad_maximum_fusion.3
  118.5 5.4 copy.49
  124.5 3.3 collective-permute-start.7
  138.2 2.9 collective-permute-start.9
  156.9 2.4 copy.47
  159.3 3.9 stack_reshape.35
  163.2 4.2 pad_maximum_fusion.2
  167.4 5.5 copy.48
  172.9 8.8 %pad_maximum_fusion = f32[4,256,2,1024]{1,0,3,2:T(4,128)} fusion(f32[4,256,1,1024]{1,0,3,2:T(4,128)} %bitcast.112, f32[4,256,1,1024]{1,0,3,2:T(4,128)} %bitcast.113), kind=kLoop, calls=%fused_computation | loop fusion | flops 2097152 | bytes 16777216 | tf_op jit(solution)/shard_map/stack | solution.py:92
  181.7 11.4 %copy.50 = f32[4,256,2,1024]{3,0,2,1:T(4,128)} copy(f32[4,256,2,1024]{1,0,3,2:T(4,128)} %pad_maximum_fusion) | data formatting | bytes 16777216 | tf_op jit(solution)/shard_map/stack | solution.py:92
  193.2 192.3 %all_to_all.36 = f32[4,512,1024]{2,0,1:T(4,128)S(1)} all-to-all(f32[4,512,1024]{2,0,1:T(4,128)} %bitcast.104), channel_id=1, replica_groups=mesh['frame'=16,'row'=2] {'frame'}, dimensions={1} | all-to-all | bytes 16777216 | tf_op jit(solution)/shard_map/all_to_all | solution.py:189
  385.5 4.9 copy.51
  404.6 4.2 copy.55
  408.8 4.9 all-to-all-start.1
  413.9 153.3 %all-to-all-done.1 = f32[64,32,1024]{2,1,0:T(8,128)} async-done(((f32[64,32,1024]{2,1,0:T(8,128)}), f32[64,32,1024]{2,1,0:T(8,128)}, u32[]{:S(2)}, u32[]{:S(2)}) %all-to-all-start.1) | async-done | bytes 8388640 | tf_op jit(solution)/shard_map/all_to_all | solution.py:191
  567.2 12.0 %mul.203 = f32[4,16,32,1024]{3,2,0,1:T(8,128)} multiply(f32[4,16,32,1024]{3,2,0,1:T(8,128)} %bitcast.39, f32[4,16,32,1024]{3,2,0,1:T(8,128)} %bitcast.39) | non-fusion elementwise | flops 2097152 | bytes 25165824 | tf_op jit(solution)/shard_map/mul | solution.py:156
  579.2 8.6 %copy.56 = f32[4,16,32,1024]{3,2,1,0:T(8,128)} copy(f32[4,16,32,1024]{3,2,0,1:T(8,128)} %bitcast.39) | data formatting | bytes 16777216 | tf_op jit(solution)/shard_map/all_to_all | solution.py:191
  587.8 4.1 copy.57
  592.0 3.9 reduce_sum.9
  596.6 72.0 %psum.7 = f32[4,10]{1,0:T(4,128)S(1)} all-reduce(f32[4,10]{1,0:T(4,128)S(1)} %fusion.56), channel_id=1, replica_groups=mesh['frame'=16,'row'=2] {'frame','row'}, use_global_device_ids=true, to_apply=%region_1.2 | all-reduce | flops 40 | bytes 320 | tf_op jit(solution)/shard_map/psum | solution.py:193
  (154 shorter events, 66.4 us)
Async XLA Ops:
  53.3 2.0 copy-start.2
  55.4 2.0 copy-start.4
  55.4 4.5 collective-permute-start
  68.2 2.0 copy-start
  70.2 3.2 collective-permute-start.1
  81.2 4.1 copy-start.1
  81.2 4.1 collective-permute-start.2
  91.1 3.9 collective-permute-start.3
  95.0 3.6 copy-start.14
  96.6 2.0 copy-start.5
  107.5 5.9 copy-start.7
  107.7 3.3 collective-permute-start.4
  111.4 2.9 collective-permute-start.5
  114.7 9.3 %collective-permute-start.6 = (f32[4,1,512]{2,1,0:T(1,128)S(1)}, f32[4,1,512]{2,1,0:T(1,128)S(1)}, u32[]{:S(2)}, u32[]{:S(2)}) collective-permute-start(f32[4,1,512]{2,1,0:T(1,128)S(1)} %slice.313), channel_id=1, source_target_pairs={{1,0},{3,2},{5,4},{7,6},{9,8},{11,10},{13,12},{15,14},{17,16},{19,... | collective-permute-start | bytes 24584 | tf_op jit(solution)/shard_map/ppermute | solution.py:21
  123.9 3.9 copy-start.6
  124.5 5.3 copy-start.15
  124.5 4.8 collective-permute-start.7
  129.7 7.2 %copy-start.9 = (f32[4,128,512]{2,1,0:T(8,128)}, f32[4,128,512]{2,1,0:T(8,128)S(1)}, u32[]{:S(2)}) copy-start(f32[4,128,512]{2,1,0:T(8,128)S(1)} %fusion.27) | copy-start | bytes 3145732
  132.9 3.8 collective-permute-start.8
  135.7 5.3 copy-start.12
  135.7 5.3 copy-start.13
  138.2 4.0 collective-permute-start.9
  142.4 4.1 collective-permute-start.10
  147.1 3.6 collective-permute-start.11
  151.0 2.1 copy-start.11
  159.3 3.9 copy-start.8
  408.8 4.9 copy-start.19
  408.8 158.4 %all-to-all-start.1 = ((f32[64,32,1024]{2,1,0:T(8,128)}), f32[64,32,1024]{2,1,0:T(8,128)}, u32[]{:S(2)}, u32[]{:S(2)}) async-start(f32[64,32,1024]{2,1,0:T(8,128)} %bitcast.102), calls=%async_computation.1 | async-start | bytes 16777216 | tf_op jit(solution)/shard_map/all_to_all | solution.py:191
  579.2 8.6 %copy-start.3 = (f32[4,16,32,1024]{3,2,0,1:T(8,128)S(1)}, f32[4,16,32,1024]{3,2,0,1:T(8,128)}, u32[]{:S(2)}) copy-start(f32[4,16,32,1024]{3,2,0,1:T(8,128)} %mul.203) | copy-start | bytes 25165828
  592.0 3.9 copy-start.17
  592.0 4.2 copy-start.16
  592.0 76.5 %copy-start.18 = (f32[4,10]{1,0:T(4,128)S(1)}, f32[4,10]{1,0:T(4,128)}, u32[]{:S(2)}) copy-start(f32[4,10]{1,0:T(4,128)} %constant.84) | copy-start | bytes 484
  (1 other events, 2.0 us)
where the time goes:
time: 680 us; the launch traced here: 670 us
  blocking collectives  264 us (39%)
  waiting for transfers between devices  161 us (24%)
  local copies, waits for them, and re-layouts  105 us (15%)
  other arithmetic  70.7 us (10%)
  matrix products  37.5 us (6%)
  starting transfers between devices  29.3 us (4%)
    all_to_all x1, blocking collectives, shards(): lax.all_to_all(planes, 'frame', split_axis=1, concat_axis=0, tiled=True)  192 us
    all_to_all x1, waiting for transfers between devices, shards(): lax.all_to_all(temporal_out, 'frame', split_axis=0, concat_axis=1, tiled=...  153 us
    psum x1, blocking collectives, shards(): totals = lax.psum(totals, ('frame', 'row'))  72 us
    dot_general x3, matrix products, spatial_inplace(): jnp.dot(block, column_matrix(width), precision=lax.Precision.HIGHEST)  36.7 us
    another operation x15, local copies, waits for them, and re-layouts, weave_axis(): stacked = jnp.stack([even_part, odd_part], axis=along + 1)  27.3 us
    ppermute x12, starting transfers between devices, shifted(): return lax.ppermute(block, axis, route)  24.4 us
    another operation x3, local copies, waits for them, and re-layouts, spatial_inplace(): jnp.stack([upper_rows, bottom], axis=2)  14.1 us
  transfers between devices with their start and end apart: 13, of which 9 were waited for; matrix products, arithmetic and copies ran while one was open for 3% of the time, Pallas kernels for 0%

commit v1 on v0

v1 whole, which is shorter than its diff:
```python
import functools

import jax
import jax.numpy as jnp
import numpy as np
from jax import lax
from jax.experimental import pallas as pl
from jax.experimental.pallas import tpu as pltpu
from jax.sharding import PartitionSpec as P

SLEVELS = 3
TLEVELS = 3
PERIOD = 2**SLEVELS
MARGIN = 4
GROUP = 4

LIFT_ALPHA = -1.586134342
LIFT_BETA = -0.05298011854
LIFT_GAMMA = 0.8829110762
LIFT_DELTA = 0.4435068522
LIFT_ZETA = 1.149604398
STEPS = (LIFT_ALPHA, LIFT_BETA, LIFT_GAMMA, LIFT_DELTA)
SCALES = 8 * SLEVELS
MASKS = SCALES + SLEVELS
MESH = pl.DeviceIdType.MESH


def level_of(number, ceiling):
    depth_now = 1
    while number % 2 == 0 and depth_now <= ceiling:
        number = number // 2
        depth_now = depth_now + 1
    return depth_now


def space_table(levels):
    period = 2**levels
    band_table = np.zeros((period * period, 3 * levels + 1), np.float32)
    for row_pos in range(period):
        for col_pos in range(period):
            row_level = level_of(row_pos, levels)
            col_level = level_of(col_pos, levels)
            finest = min(row_level, col_level)
            if finest > levels:
                column = 3 * levels
            elif row_level == col_level:
                column = 3 * (finest - 1) + 2
            elif row_level == finest:
                column = 3 * (finest - 1)
            else:
                column = 3 * (finest - 1) + 1
            band_table[row_pos * period + col_pos, column] = 1.0
    return band_table


def time_table(levels):
    period = 2**levels
    band_table = np.zeros((period, levels + 1), np.float32)
    for number in range(period):
        band_table[number, level_of(number, levels) - 1] = 1.0
    return band_table


def band_means(totals, frames_all, rows_all, cols_all, levels_s, levels_t):
    space_share = space_table(levels_s).sum(0) / float((2**levels_s) ** 2)
    time_share = time_table(levels_t).sum(0) / float(2**levels_t)
    counts = (
        float(frames_all) * float(rows_all) * float(cols_all) * np.outer(time_share, space_share)
    )
    return totals / jnp.asarray(counts, jnp.float32)


def shifted(block, axis, distance):
    devices = range(lax.axis_size(axis))
    route = [(i - distance, i) for i in devices if i - distance in devices]
    return lax.ppermute(block, axis, route)


def lane_table(width):
    lane = np.arange(width)
    table = np.zeros((MASKS + SLEVELS, width), np.float64)
    for level in range(SLEVELS):
        s = 2**level
        odd = lane % (2 * s) == s
        even = lane % (2 * s) == 0
        for step, factor in enumerate(STEPS):
            left = factor * (odd if step % 2 == 0 else even)
            right = left.copy()
            if step % 2 == 0:
                left[width - s], right[width - s] = 2 * factor, 0.0
            else:
                left[0], right[0] = 0.0, 2 * factor
            table[8 * level + 2 * step] = left
            table[8 * level + 2 * step + 1] = right
        table[SCALES + level] = np.where(even, LIFT_ZETA, np.where(odd, 1.0 / LIFT_ZETA, 1.0))
        table[MASKS + level] = lane % s == 0
    return table.astype(np.float32)


def spatial_kernel(tab_ref, x_ref, o_ref, buf):
    groups, width = buf.shape[1:]
    inner = groups - 2 * MARGIN
    row = lax.axis_index("row")
    at_top = row == 0
    at_bottom = row == lax.axis_size("row") - 1
    tiles = groups // 8

    for level in range(SLEVELS):
        s = 2**level
        source = x_ref.at[0] if level == 0 else buf

        def columns(i, carry, level=level, s=s, source=source):
            phase = (i // tiles) * s
            q = pl.ds(pl.multiple_of((i % tiles) * 8, 8), 8)
            x = source[phase, q, :]
            for step in range(4):
                k = 8 * level + 2 * step
                before = pltpu.roll(x, s, 1)
                after = pltpu.roll(x, width - s, 1)
                x = x + tab_ref[pl.ds(k, 1), :] * before + tab_ref[pl.ds(k + 1, 1), :] * after
            buf[phase, q, :] = x * tab_ref[pl.ds(SCALES + level, 1), :]
            return carry

        lax.fori_loop(0, (PERIOD // s) * tiles, columns, 0)

        def rows(i, carry, level=level, s=s):
            lanes = pl.ds(pl.multiple_of(i * 128, 128), 128)
            mask = tab_ref[pl.ds(MASKS + level, 1), lanes]
            x = {p: buf[p, :, lanes] for p in range(0, PERIOD, s)}
            index = lax.broadcasted_iota(jnp.int32, (groups, 128), 0)
            first = jnp.logical_and(index == MARGIN, at_top)
            last = jnp.logical_and(index == MARGIN + inner - 1, at_bottom)
            for step, factor in enumerate(STEPS):
                c = factor * mask
                if step % 2 == 0:
                    for p in range(s, PERIOD, 2 * s):
                        if p + s < PERIOD:
                            after = x[p + s]
                        else:
                            after = jnp.where(last, x[p - s], pltpu.roll(x[0], groups - 1, 0))
                        x[p] = x[p] + c * (x[p - s] + after)
                else:
                    for p in range(0, PERIOD, 2 * s):
                        if p > 0:
                            before = x[p - s]
                        else:
                            before = jnp.where(first, x[s], pltpu.roll(x[PERIOD - s], 1, 0))
                        x[p] = x[p] + c * (before + x[p + s])
            up = jnp.where(mask > 0, LIFT_ZETA, 1.0)
            down = jnp.where(mask > 0, 1.0 / LIFT_ZETA, 1.0)
            for p in x:
                low = p % (2 * s) == 0
                value = x[p] * (up if low else down)
                if low and level < SLEVELS - 1:
                    buf[p, :, lanes] = value
                else:
                    o_ref[0, p, :, lanes] = value[MARGIN : MARGIN + inner]
            return carry

        lax.fori_loop(0, width // 128, rows, 0)


def spatial(footage):
    frames, rows, width = footage.shape
    edge = MARGIN * PERIOD
    above = shifted(footage[:, -edge:], "row", 1)
    below = shifted(footage[:, :edge], "row", -1)
    groups = rows // PERIOD + 2 * MARGIN
    x = jnp.concatenate([above, footage, below], axis=1)
    x = x.reshape(frames, groups, PERIOD, width).transpose(0, 2, 1, 3)
    inner = rows // PERIOD
    table = jnp.asarray(lane_table(width))
    return pl.pallas_call(
        spatial_kernel,
        grid=(frames,),
        out_shape=jax.ShapeDtypeStruct((frames, PERIOD, inner, width), jnp.float32),
        in_specs=[
            pl.BlockSpec(table.shape, lambda i: (0, 0)),
            pl.BlockSpec((1, PERIOD, groups, width), lambda i: (i, 0, 0, 0)),
        ],
        out_specs=pl.BlockSpec((1, PERIOD, inner, width), lambda i: (i, 0, 0, 0)),
        scratch_shapes=[pltpu.VMEM((PERIOD, groups, width), jnp.float32)],
        compiler_params=pltpu.CompilerParams(vmem_limit_bytes=50 * 2**20),
    )(table, x)


def outgoing(f):
    o = {i: f[i] - 0.5 * (f[i - 1] + f[i + 1]) for i in range(1, 14, 2)}
    a = {i: f[i] + 0.25 * (o[i - 1] + o[i + 1]) for i in range(2, 13, 2)}
    p6 = a[6] - 0.5 * (a[4] + a[8])
    p10 = a[10] - 0.5 * (a[8] + a[12])
    b8 = a[8] + 0.25 * (p6 + p10)
    to_before = (f[0], o[1], a[2] - 0.5 * a[4])
    to_after = (
        f[15] - 0.5 * f[14],
        f[14] + 0.25 * o[13] - 0.5 * a[12],
        a[12] + 0.25 * p10 - 0.5 * b8,
    )
    return to_before, to_after


def temporal(f, before, after, is_first, is_last):
    o = {i: f[i] - 0.5 * (f[i - 1] + f[i + 1]) for i in range(1, 14, 2)}
    f16 = jnp.where(is_last, f[14], after[0])
    o[15] = f[15] - 0.5 * (f[14] + f16)
    o[-1] = jnp.where(is_first, o[1], before[0] - 0.5 * f[0])
    a = {i: f[i] + 0.25 * (o[i - 1] + o[i + 1]) for i in range(0, 16, 2)}
    a16 = jnp.where(is_last, a[12], after[0] + 0.25 * (o[15] + after[1]))
    a[16] = a16
    p = {i: a[i] - 0.5 * (a[i - 2] + a[i + 2]) for i in range(2, 16, 4)}
    p[-2] = jnp.where(is_first, p[2], before[1] + 0.25 * o[-1] - 0.5 * a[0])
    b = {i: a[i] + 0.25 * (p[i - 2] + p[i + 2]) for i in range(0, 16, 4)}
    b[16] = jnp.where(is_last, b[8], a16 + 0.25 * (p[14] + after[2] - 0.5 * a16))
    d4 = b[4] - 0.5 * (b[0] + b[8])
    d12 = b[12] - 0.5 * (b[8] + b[16])
    dm4 = jnp.where(is_first, d4, before[2] + 0.25 * p[-2] - 0.5 * b[0])
    out = {i: o[i] for i in range(1, 16, 2)}
    out.update({i: p[i] for i in range(2, 16, 4)})
    out[4], out[12] = d4, d12
    out[0] = b[0] + 0.25 * (dm4 + d4)
    out[8] = b[8] + 0.25 * (d4 + d12)
    return out


def exchange_kernel(x_ref, o_ref, sums_ref, held, from_before, from_after, to_before, to_after,
                    f_send, f_recv, f_own, h_send, h_recv, r_send, r_recv, r_own):
    frames, phases, inner, width = x_ref.shape
    part = inner // GROUP
    me = lax.axis_index("frame")
    count = lax.axis_size("frame")
    member = me % GROUP
    base = me - member
    is_first = base == 0
    is_last = base == count - GROUP
    previous = (me + count - GROUP) % count
    following = (me + GROUP) % count
    peers = [base + (member + k) % GROUP for k in range(1, GROUP)]

    barrier = pltpu.get_barrier_semaphore()
    for peer in peers + [previous, following]:
        pl.semaphore_signal(barrier, inc=1, device_id={"frame": peer}, device_id_type=MESH)
    pl.semaphore_wait(barrier, GROUP + 1)

    def part_of(device):
        return pl.ds(pl.multiple_of((device % GROUP) * part, 8), part)

    def frames_of(device):
        return pl.ds((device % GROUP) * frames, frames)

    def forward(c, k):
        peer = peers[k]
        return pltpu.make_async_remote_copy(
            src_ref=x_ref.at[:, c, part_of(peer), :],
            dst_ref=held.at[frames_of(me), c],
            send_sem=f_send.at[k, c],
            recv_sem=f_recv.at[k, c],
            device_id={"frame": peer},
            device_id_type=MESH,
        )

    def forward_own(c):
        return pltpu.make_async_copy(
            x_ref.at[:, c, part_of(me), :], held.at[frames_of(me), c], f_own.at[c]
        )

    def halo(c, side):
        return pltpu.make_async_remote_copy(
            src_ref=(to_before if side == 0 else to_after).at[c],
            dst_ref=(from_after if side == 0 else from_before).at[c],
            send_sem=h_send.at[side, c],
            recv_sem=h_recv.at[side, c],
            device_id={"frame": previous if side == 0 else following},
            device_id_type=MESH,
        )

    def back(c, k):
        peer = peers[k]
        return pltpu.make_async_remote_copy(
            src_ref=held.at[frames_of(peer), c],
            dst_ref=o_ref.at[:, c, part_of(me), :],
            send_sem=r_send.at[k, c],
            recv_sem=r_recv.at[k, c],
            device_id={"frame": peer},
            device_id_type=MESH,
        )

    def back_own(c):
        return pltpu.make_async_copy(
            held.at[frames_of(me), c], o_ref.at[:, c, part_of(me), :], r_own.at[c]
        )

    def start_forward(c, carry):
        for k in range(GROUP - 1):
            forward(c, k).start()
        forward_own(c).start()
        return carry

    lax.fori_loop(0, phases, start_forward, 0)
    total = GROUP * frames
    strip = 128
    strips = width // strip

    def send_halo(c):
        for k in range(GROUP - 1):
            forward(c, k).wait_recv()
        forward_own(c).wait()

        def tile(i, carry):
            lanes = pl.ds(pl.multiple_of(i * strip, strip), strip)
            left, right = outgoing([held[n, c, :, lanes] for n in range(total)])
            for j in range(TLEVELS):
                to_before[c, j, :, lanes] = left[j]
                to_after[c, j, :, lanes] = right[j]
            return carry

        lax.fori_loop(0, strips, tile, 0)
        for side in range(2):
            halo(c, side).start()

    def finish(c):
        for side in range(2):
            halo(c, side).wait_recv()

        def tile(i, carry):
            lanes = pl.ds(pl.multiple_of(i * strip, strip), strip)
            f = [held[n, c, :, lanes] for n in range(total)]
            before = [from_before[c, j, :, lanes] for j in range(TLEVELS)]
            after = [from_after[c, j, :, lanes] for j in range(TLEVELS)]
            out = temporal(f, before, after, is_first, is_last)
            sums = [None] * (TLEVELS + 1)
            for n in range(total):
                held[n, c, :, lanes] = out[n]
                t = level_of(n % 2**TLEVELS, TLEVELS) - 1
                square = out[n] * out[n]
                sums[t] = square if sums[t] is None else sums[t] + square
            for t in range(TLEVELS + 1):
                sums_ref[t, c, :, lanes] = jnp.sum(
                    sums[t].reshape(part // 8, 8, strip), axis=0
                )
            return carry

        lax.fori_loop(0, strips, tile, 0)
        for k in range(GROUP - 1):
            back(c, k).start()
        back_own(c).start()

    send_halo(0)

    def middle(c, carry):
        send_halo(c)
        finish(c - 1)
        return carry

    lax.fori_loop(1, phases, middle, 0)
    finish(phases - 1)

    def drain(c, carry):
        for k in range(GROUP - 1):
            forward(c, k).wait_send()
            back(c, k).wait()
        for side in range(2):
            halo(c, side).wait_send()
        back_own(c).wait()
        return carry

    lax.fori_loop(0, phases, drain, 0)


def exchange(planes):
    frames, phases, inner, width = planes.shape
    part = inner // GROUP
    any_space = pl.BlockSpec(memory_space=pl.ANY)
    halo_buffer = pltpu.VMEM((phases, TLEVELS, part, width), jnp.float32)
    dma = pltpu.SemaphoreType.DMA
    return pl.pallas_call(
        exchange_kernel,
        out_shape=(
            jax.ShapeDtypeStruct(planes.shape, jnp.float32),
            jax.ShapeDtypeStruct((TLEVELS + 1, phases, 8, width), jnp.float32),
        ),
        in_specs=[any_space],
        out_specs=(any_space, pl.BlockSpec(memory_space=pltpu.VMEM)),
        scratch_shapes=[
            pltpu.VMEM((GROUP * frames, phases, part, width), jnp.float32),
            halo_buffer, halo_buffer, halo_buffer, halo_buffer,
            dma((GROUP - 1, phases)), dma((GROUP - 1, phases)), dma((phases,)),
            dma((2, phases)), dma((2, phases)),
            dma((GROUP - 1, phases)), dma((GROUP - 1, phases)), dma((phases,)),
        ],
        compiler_params=pltpu.CompilerParams(
            collective_id=0, has_side_effects=True, vmem_limit_bytes=50 * 2**20
        ),
    )(planes)


def shards(footage):
    frames, rows, width = footage.shape
    planes = spatial(footage)
    coeffs, sums = exchange(planes)
    coeffs = coeffs.transpose(0, 2, 1, 3).reshape(frames, rows, width)
    pattern = sums.sum(axis=2).reshape(TLEVELS + 1, PERIOD, width // PERIOD, PERIOD).sum(axis=2)
    pattern = pattern.reshape(TLEVELS + 1, PERIOD * PERIOD)
    totals = jnp.dot(
        pattern, jnp.asarray(space_table(SLEVELS), jnp.float32), precision=lax.Precision.HIGHEST
    )
    totals = lax.psum(totals, ("frame", "row"))
    means = band_means(
        totals,
        frames * lax.axis_size("frame"),
        rows * lax.axis_size("row"),
        width,
        SLEVELS,
        TLEVELS,
    )
    return (coeffs, means)


def solution(mesh):
    return jax.shard_map(
        shards,
        mesh=mesh,
        in_specs=(P("frame", "row", None),),
        out_specs=(P("frame", "row", None), P()),
        check_vma=False,
    )
```

time: 680 us -> 450 us (0.66); the launches traced: 670 us -> 450 us
  Pallas kernels: 0 us -> 367 us
  blocking collectives: 264 us -> 38.2 us
  waiting for transfers between devices: 161 us -> 2.5 us
  local copies, waits for them, and re-layouts: 105 us -> 27 us
  other arithmetic: 70.7 us -> 9.94 us
  matrix products: 37.5 us -> 0.13 us
  starting transfers between devices: 29.3 us -> 3.72 us
    pallas_call x0 -> x2, Pallas kernels: none -> 367 us  [the longest x1 189 us: exchange(): pl.pallas_call(exchange_kernel, out_shape=(jax.ShapeDtypeStruct(planes.sh...]
    all_to_all x1 -> x0, blocking collectives: 192 us -> none  [shards(): lax.all_to_all(planes, 'frame', split_axis=1, concat_axis=0, tiled=True)]
    all_to_all x1 -> x0, waiting for transfers between devices: 153 us -> none  [shards(): lax.all_to_all(temporal_out, 'frame', split_axis=0, concat_axis=1, tiled=...]
    another operation x18 -> x0, local copies, waits for them, and re-layouts: 41.4 us -> none  [the longest x15 27.3 us: weave_axis(): stacked = jnp.stack([even_part, odd_part], axis=along + 1)]
    dot_general x7 -> x1, matrix products: 37.5 us -> 0.13 us  [shards(): jnp.dot(pattern, jnp.asarray(space_table(SLEVELS), jnp.float32), precisio...]
    psum x1, blocking collectives: 72 us -> 38.2 us  [shards(): totals = lax.psum(totals, ('frame', 'row'))]
    slice x35 -> x1, local copies, waits for them, and re-layouts: 22.9 us -> 1.31 us  [spatial(): above = shifted(footage[:, -edge:], 'row', 1)]
    another operation x13 -> x0, other arithmetic: 21.6 us -> none  [the longest x10 11.3 us: weave_axis(): stacked = jnp.stack([even_part, odd_part], axis=along + 1)]
  transfers between devices with their start and end apart: 13 -> 2, of which waited for: 9 -> 2; matrix products, arithmetic and copies ran while one was open for 3% -> 0% of each run, Pallas kernels for 0% -> 0%
where the time goes in v1:
time: 450 us
  Pallas kernels  367 us (82%)
  blocking collectives  38.2 us (8%)
  local copies, waits for them, and re-layouts  27 us (6%)
  other arithmetic  9.94 us (2%)
    pallas_call x1, Pallas kernels, exchange(): pl.pallas_call(exchange_kernel, out_shape=(jax.ShapeDtypeStruct(planes.sh...  189 us
    pallas_call x1, Pallas kernels, spatial(): pl.pallas_call(spatial_kernel, grid=(frames,), out_shape=jax.ShapeDtypeSt...  179 us
    psum x1, blocking collectives, shards(): totals = lax.psum(totals, ('frame', 'row'))  38.2 us
    reshape x1, local copies, waits for them, and re-layouts, spatial(): x = x.reshape(frames, groups, PERIOD, width).transpose(0, 2, 1, 3)  12.8 us
    transpose x1, local copies, waits for them, and re-layouts, shards(): coeffs = coeffs.transpose(0, 2, 1, 3).reshape(frames, rows, width)  11.6 us
  transfers between devices with their start and end apart: 2, of which 2 were waited for; matrix products, arithmetic and copies ran while one was open for 0% of the time, Pallas kernels for 0%

profile of v1, /device:TPU:0, one launch (start us, length us, event | category | flops | bytes accessed | tf_op | source)
XLA Modules:
  0.0 449.7 jit_solution(12633987438502957078)
XLA Ops:
  0.6 1.3 fusion
  1.9 2.4 collective-permute-start
  4.4 1.3 collective-permute-start.1
  5.7 0.2 collective-permute-done
  5.9 2.3 collective-permute-done.1
  8.2 8.9 %maximum_bitcast_fusion = f32[4,72,8,1024]{3,2,1,0:T(8,128)} fusion(f32[4,32,1024]{2,1,0:T(8,128)S(1)} %collective-permute-done.1, f32[4,512,1024]{2,1,0:T(8,128)} %param.4, f32[4,32,1024]{2,1,0:T(8,128)S(1)} %collective-permute-done), kind=kLoop, calls=%fused_computation | loop fusion | flops 4718592 | bytes 18874368 | tf_op jit(solution)/shard_map/reshape | solution.py:170
  17.1 0.0 copy-start
  17.1 12.8 %copy.10 = f32[4,72,8,1024]{3,1,2,0:T(8,128)} copy(f32[4,72,8,1024]{3,2,1,0:T(8,128)} %maximum_bitcast_fusion) | data formatting | bytes 18874368 | tf_op jit(solution)/shard_map/reshape | solution.py:170
  30.0 0.0 copy-done
  30.0 178.8 %shard_map.59.x_ref = f32[4,8,64,1024]{3,2,1,0:T(8,128)} custom-call(f32[30,1024]{1,0:T(8,128)S(1)} %copy-done, f32[4,8,72,1024]{3,2,1,0:T(8,128)} %bitcast.11), custom_call_target="tpu_custom_call" | custom-call | tf_op jit(solution)/shard_map/pallas_call | solution.py:173
  208.7 188.7 %shard_map.60 = (f32[4,8,64,1024]{3,2,1,0:T(8,128)}, f32[4,8,8,1024]{3,2,1,0:T(8,128)S(1)}) custom-call(f32[4,8,64,1024]{3,2,1,0:T(8,128)} %shard_map.59.x_ref), custom_call_target="tpu_custom_call" | custom-call | tf_op jit(solution)/shard_map/pallas_call | solution.py:375
  397.4 0.0 copy-start.1
  397.5 0.0 copy-start.2
  397.5 11.6 %copy.11 = f32[4,64,8,1024]{3,2,1,0:T(8,128)} copy(f32[4,64,8,1024]{3,1,2,0:T(8,128)} %bitcast.13) | data formatting | bytes 16777216 | tf_op jit(solution)/shard_map/transpose | solution.py:400
  409.1 0.2 reduce_sum.18
  409.4 1.1 reshape.18
  410.5 0.2 reduce_sum.19
  410.7 0.1 reshape.19
  410.8 0.0 copy-done.1
  410.8 0.1 fusion.1
  410.9 38.2 %psum.7 = f32[4,10]{1,0:T(4,128)S(1)} all-reduce(f32[4,10]{1,0:T(4,128)S(1)} %fusion.1), channel_id=1, replica_groups=mesh['frame'=16,'row'=2] {'frame','row'}, use_global_device_ids=true, to_apply=%region_2.0 | all-reduce | flops 40 | bytes 320 | tf_op jit(solution)/shard_map/psum | solution.py:406
  449.1 0.0 copy-done.2
  449.1 0.6 multiply
Async XLA Ops:
  1.9 3.9 collective-permute-start
  4.4 3.8 collective-permute-start.1
  17.1 12.8 %copy-start = (f32[30,1024]{1,0:T(8,128)S(1)}, f32[30,1024]{1,0:T(8,128)}, u32[]{:S(2)}) copy-start(f32[30,1024]{1,0:T(8,128)} %constant.8.clone.tab_ref) | copy-start | bytes 368644
  397.4 13.3 %copy-start.1 = (f32[64,10]{1,0:T(8,128)S(1)}, f32[64,10]{1,0:T(8,128)}, u32[]{:S(2)}) copy-start(f32[64,10]{1,0:T(8,128)} %constant.9.clone) | copy-start | bytes 7684
  397.5 51.6 %copy-start.2 = (f32[4,10]{1,0:T(4,128)S(1)}, f32[4,10]{1,0:T(4,128)}, u32[]{:S(2)}) copy-start(f32[4,10]{1,0:T(4,128)} %constant.12) | copy-start | bytes 484

commit v2 on v1

--- a/solution.py
+++ b/solution.py
@@ -20,8 +20,9 @@
 LIFT_DELTA = 0.4435068522
 LIFT_ZETA = 1.149604398
 STEPS = (LIFT_ALPHA, LIFT_BETA, LIFT_GAMMA, LIFT_DELTA)
-SCALES = 8 * SLEVELS
-MASKS = SCALES + SLEVELS
+REACH = 4
+TAPS = 2 * REACH + 1
+MASKS = TAPS * SLEVELS
 MESH = pl.DeviceIdType.MESH
 
 
@@ -76,49 +77,83 @@
     return lax.ppermute(block, axis, route)
 
 
+def lifted_identity(size):
+    x = np.eye(size)
+    after = np.concatenate([np.arange(2, size, 2), [size - 2]])
+    before = np.concatenate([[1], np.arange(1, size - 1, 2)])
+    even, odd = np.arange(0, size, 2), np.arange(1, size, 2)
+    x[:, odd] += LIFT_ALPHA * (x[:, even] + x[:, after])
+    x[:, even] += LIFT_BETA * (x[:, before] + x[:, odd])
+    x[:, odd] += LIFT_GAMMA * (x[:, even] + x[:, after])
+    x[:, even] += LIFT_DELTA * (x[:, before] + x[:, odd])
+    x[:, even] *= LIFT_ZETA
+    x[:, odd] *= 1.0 / LIFT_ZETA
+    return x
+
+
 def lane_table(width):
-    lane = np.arange(width)
     table = np.zeros((MASKS + SLEVELS, width), np.float64)
     for level in range(SLEVELS):
         s = 2**level
-        odd = lane % (2 * s) == s
-        even = lane % (2 * s) == 0
-        for step, factor in enumerate(STEPS):
-            left = factor * (odd if step % 2 == 0 else even)
-            right = left.copy()
-            if step % 2 == 0:
-                left[width - s], right[width - s] = 2 * factor, 0.0
-            else:
-                left[0], right[0] = 0.0, 2 * factor
-            table[8 * level + 2 * step] = left
-            table[8 * level + 2 * step + 1] = right
-        table[SCALES + level] = np.where(even, LIFT_ZETA, np.where(odd, 1.0 / LIFT_ZETA, 1.0))
-        table[MASKS + level] = lane % s == 0
+        size = width // s
+        matrix = lifted_identity(size)
+        table[TAPS * level + REACH] = 1.0
+        for k in range(-REACH, REACH + 1):
+            n = np.arange(max(0, -k), min(size, size - k))
+            row = np.zeros(size)
+            row[n] = matrix[n + k, n]
+            table[TAPS * level + REACH + k, ::s] = row
+        table[MASKS + level, ::s] = 1.0
     return table.astype(np.float32)
 
 
-def spatial_kernel(tab_ref, x_ref, o_ref, buf):
+def spatial_kernel(tab_ref, x_ref, halo_ref, o_ref, xin, buf, x_sem, h_sem):
     groups, width = buf.shape[1:]
     inner = groups - 2 * MARGIN
     row = lax.axis_index("row")
     at_top = row == 0
     at_bottom = row == lax.axis_size("row") - 1
-    tiles = groups // 8
-
+    frame = pl.program_id(0)
+    slot = frame % 2
+
+    def copies(f, slot):
+        for p in range(PERIOD):
+            yield pltpu.make_async_copy(
+                x_ref.at[f, :, p, :], xin.at[slot, p, pl.ds(0, inner), :], x_sem.at[slot, p]
+            )
+            yield pltpu.make_async_copy(
+                halo_ref.at[f, p], xin.at[slot, p, pl.ds(inner, 2 * MARGIN), :], h_sem.at[slot, p]
+            )
+
+    @pl.when(frame == 0)
+    def _():
+        for copy in copies(frame, slot):
+            copy.start()
+
+    @pl.when(frame + 1 < pl.num_programs(0))
+    def _():
+        for copy in copies(frame + 1, 1 - slot):
+            copy.start()
+
+    for copy in copies(frame, slot):
+        copy.wait()
+
+    tile = 24
+    tiles = groups // tile
     for level in range(SLEVELS):
         s = 2**level
-        source = x_ref.at[0] if level == 0 else buf
+        source = xin.at[slot] if level == 0 else buf
 
         def columns(i, carry, level=level, s=s, source=source):
             phase = (i // tiles) * s
-            q = pl.ds(pl.multiple_of((i % tiles) * 8, 8), 8)
+            q = pl.ds(pl.multiple_of((i % tiles) * tile, 8), tile)
             x = source[phase, q, :]
-            for step in range(4):
-                k = 8 * level + 2 * step
-                before = pltpu.roll(x, s, 1)
-                after = pltpu.roll(x, width - s, 1)
-                x = x + tab_ref[pl.ds(k, 1), :] * before + tab_ref[pl.ds(k + 1, 1), :] * after
-            buf[phase, q, :] = x * tab_ref[pl.ds(SCALES + level, 1), :]
+            y = x * tab_ref[pl.ds(TAPS * level + REACH, 1), :]
+            for k in range(1, REACH + 1):
+                for sign in (-1, 1):
+                    moved = pltpu.roll(x, (-sign * k * s) % width, 1)
+                    y = y + moved * tab_ref[pl.ds(TAPS * level + REACH + sign * k, 1), :]
+            buf[phase, q, :] = y
             return carry
 
         lax.fori_loop(0, (PERIOD // s) * tiles, columns, 0)
@@ -128,8 +163,8 @@
             mask = tab_ref[pl.ds(MASKS + level, 1), lanes]
             x = {p: buf[p, :, lanes] for p in range(0, PERIOD, s)}
             index = lax.broadcasted_iota(jnp.int32, (groups, 128), 0)
-            first = jnp.logical_and(index == MARGIN, at_top)
-            last = jnp.logical_and(index == MARGIN + inner - 1, at_bottom)
+            first = jnp.logical_and(index == 0, at_top)
+            last = jnp.logical_and(index == inner - 1, at_bottom)
             for step, factor in enumerate(STEPS):
                 c = factor * mask
                 if step % 2 == 0:
@@ -154,7 +189,7 @@
                 if low and level < SLEVELS - 1:
                     buf[p, :, lanes] = value
                 else:
-                    o_ref[0, p, :, lanes] = value[MARGIN : MARGIN + inner]
+                    o_ref[0, p, :, lanes] = value[:inner]
             return carry
 
         lax.fori_loop(0, width // 128, rows, 0)
@@ -163,25 +198,28 @@
 def spatial(footage):
     frames, rows, width = footage.shape
     edge = MARGIN * PERIOD
+    inner = rows // PERIOD
+    groups = inner + 2 * MARGIN
     above = shifted(footage[:, -edge:], "row", 1)
     below = shifted(footage[:, :edge], "row", -1)
-    groups = rows // PERIOD + 2 * MARGIN
-    x = jnp.concatenate([above, footage, below], axis=1)
-    x = x.reshape(frames, groups, PERIOD, width).transpose(0, 2, 1, 3)
-    inner = rows // PERIOD
+    halo = jnp.concatenate([below, above], axis=1)
+    halo = halo.reshape(frames, 2 * MARGIN, PERIOD, width).transpose(0, 2, 1, 3)
     table = jnp.asarray(lane_table(width))
+    any_space = pl.BlockSpec(memory_space=pl.ANY)
     return pl.pallas_call(
         spatial_kernel,
         grid=(frames,),
         out_shape=jax.ShapeDtypeStruct((frames, PERIOD, inner, width), jnp.float32),
-        in_specs=[
-            pl.BlockSpec(table.shape, lambda i: (0, 0)),
-            pl.BlockSpec((1, PERIOD, groups, width), lambda i: (i, 0, 0, 0)),
+        in_specs=[pl.BlockSpec(table.shape, lambda i: (0, 0)), any_space, any_space],
+        out_specs=pl.BlockSpec((1, PERIOD, inner, width), lambda i: (i, 0, 0, 0)),
+        scratch_shapes=[
+            pltpu.VMEM((2, PERIOD, groups, width), jnp.float32),
+            pltpu.VMEM((PERIOD, groups, width), jnp.float32),
+            pltpu.SemaphoreType.DMA((2, PERIOD)),
+            pltpu.SemaphoreType.DMA((2, PERIOD)),
         ],
-        out_specs=pl.BlockSpec((1, PERIOD, inner, width), lambda i: (i, 0, 0, 0)),
-        scratch_shapes=[pltpu.VMEM((PERIOD, groups, width), jnp.float32)],
         compiler_params=pltpu.CompilerParams(vmem_limit_bytes=50 * 2**20),
-    )(table, x)
+    )(table, footage.reshape(frames, inner, PERIOD, width), halo)
 
 
 def outgoing(f):
@@ -393,6 +431,87 @@
     )(planes)
 
 
+def total_kernel(x_ref, o_ref, inbox, send, recv):
+    strips = lax.axis_size("row")
+    count = lax.axis_size("frame") * strips
+    me = lax.axis_index("frame") * strips + lax.axis_index("row")
+
+    def place(device):
+        return {"frame": device // strips, "row": device % strips}
+
+    barrier = pltpu.get_barrier_semaphore()
+
+    def greet(j, carry):
+        pl.semaphore_signal(
+            barrier, inc=1, device_id=place((me + j) % count), device_id_type=MESH
+        )
+        return carry
+
+    lax.fori_loop(1, count, greet, 0)
+    pl.semaphore_wait(barrier, count - 1)
+
+    def to_peer(j):
+        return pltpu.make_async_remote_copy(
+            src_ref=x_ref,
+            dst_ref=inbox.at[me],
+            send_sem=send.at[j],
+            recv_sem=recv.at[me],
+            device_id=place((me + j) % count),
+            device_id_type=MESH,
+        )
+
+    def start(j, carry):
+        to_peer(j).start()
+        return carry
+
+    lax.fori_loop(1, count, start, 0)
+
+    inbox[me] = x_ref[...]
+
+    def arrive(j, carry):
+        source = (me + j) % count
+        pltpu.make_async_remote_copy(
+            src_ref=x_ref,
+            dst_ref=inbox.at[source],
+            send_sem=send.at[j],
+            recv_sem=recv.at[source],
+            device_id=place(source),
+            device_id_type=MESH,
+        ).wait_recv()
+        return carry
+
+    lax.fori_loop(1, count, arrive, 0)
+    o_ref[...] = lax.fori_loop(
+        1, count, lambda j, total: total + inbox[j], inbox[0]
+    )
+
+    def drain(j, carry):
+        to_peer(j).wait_send()
+        return carry
+
+    lax.fori_loop(1, count, drain, 0)
+
+
+def total_over_devices(values):
+    count = lax.axis_size("frame") * lax.axis_size("row")
+    padded = jnp.zeros((8, 128), jnp.float32)
+    padded = padded.at[: values.shape[0], : values.shape[1]].set(values)
+    vmem = pl.BlockSpec(memory_space=pltpu.VMEM)
+    total = pl.pallas_call(
+        total_kernel,
+        out_shape=jax.ShapeDtypeStruct((8, 128), jnp.float32),
+        in_specs=[vmem],
+        out_specs=vmem,
+        scratch_shapes=[
+            pltpu.VMEM((count, 8, 128), jnp.float32),
+            pltpu.SemaphoreType.DMA((count,)),
+            pltpu.SemaphoreType.DMA((count,)),
+        ],
+        compiler_params=pltpu.CompilerParams(collective_id=1, has_side_effects=True),
+    )(padded)
+    return total[: values.shape[0], : values.shape[1]]
+
+
 def shards(footage):
     frames, rows, width = footage.shape
     planes = spatial(footage)
@@ -403,7 +522,7 @@
     totals = jnp.dot(
         pattern, jnp.asarray(space_table(SLEVELS), jnp.float32), precision=lax.Precision.HIGHEST
     )
-    totals = lax.psum(totals, ("frame", "row"))
+    totals = total_over_devices(totals)
     means = band_means(
         totals,
         frames * lax.axis_size("frame"),

time: 450 us -> 283 us (0.63)
  Pallas kernels: 367 us -> 258 us
  blocking collectives: 38.2 us -> 0 us
  local copies, waits for them, and re-layouts: 27 us -> 16.3 us
  other arithmetic: 9.94 us -> 1.79 us
    pallas_call x1, Pallas kernels: 179 us -> 58.8 us  [spatial(): pl.pallas_call(spatial_kernel, grid=(frames,), out_shape=jax.ShapeDtypeSt...]
    psum x1 -> x0, blocking collectives: 38.2 us -> none  [shards(): totals = lax.psum(totals, ('frame', 'row'))]
    reshape x1, local copies, waits for them, and re-layouts: 12.8 us -> 0.61 us  [spatial(): halo = halo.reshape(frames, 2 * MARGIN, PERIOD, width).transpose(0, 2, 1, 3)]
    pallas_call x0 -> x1, Pallas kernels: none -> 9.8 us  [total_over_devices(): pl.pallas_call(total_kernel, out_shape=jax.ShapeDtypeStruct((8, 128), jnp...]
    reshape x1, other arithmetic: 8.93 us -> 0.1 us  [spatial(): halo = halo.reshape(frames, 2 * MARGIN, PERIOD, width).transpose(0, 2, 1, 3)]
  transfers between devices with their start and end apart: 2 -> 2, of which waited for: 2 -> 1; matrix products, arithmetic and copies ran while one was open for 0% -> 0% of each run, Pallas kernels for 0% -> 0%
where the time goes in v2:
time: 283 us
  Pallas kernels  258 us (91%)
  local copies, waits for them, and re-layouts  16.3 us (6%)
  starting transfers between devices  4.38 us (2%)
    pallas_call x1, Pallas kernels, exchange(): pl.pallas_call(exchange_kernel, out_shape=(jax.ShapeDtypeStruct(planes.sh...  190 us
    pallas_call x1, Pallas kernels, spatial(): pl.pallas_call(spatial_kernel, grid=(frames,), out_shape=jax.ShapeDtypeSt...  58.8 us
    transpose x1, local copies, waits for them, and re-layouts, shards(): coeffs = coeffs.transpose(0, 2, 1, 3).reshape(frames, rows, width)  11.6 us
    pallas_call x1, Pallas kernels, total_over_devices(): pl.pallas_call(total_kernel, out_shape=jax.ShapeDtypeStruct((8, 128), jnp...  9.8 us
  transfers between devices with their start and end apart: 2, of which 1 were waited for; matrix products, arithmetic and copies ran while one was open for 0% of the time, Pallas kernels for 0%

profile of v2, /device:TPU:0, one launch (start us, length us, event | category | flops | bytes accessed | tf_op | source)
XLA Modules:
  0.0 283.0 jit_solution(14741695017577329706)
XLA Ops:
  0.6 1.3 fusion
  1.9 1.3 collective-permute-start
  3.2 3.1 %collective-permute-start.1 = (f32[4,32,1024]{2,1,0:T(8,128)S(1)}, f32[4,32,1024]{2,1,0:T(8,128)S(1)}, u32[]{:S(2)}, u32[]{:S(2)}) collective-permute-start(f32[4,32,1024]{2,1,0:T(8,128)S(1)} %get-tuple-element.19), channel_id=1, source_target_pairs={{0,1},{2,3},{4,5},{6,7},{8,9},{10,11},{12,13},{14,15},{16,17},{18,... | collective-permute-start | bytes 1572872 | tf_op jit(solution)/shard_map/ppermute | solution.py:77
  6.3 0.0 collective-permute-done
  6.4 1.5 collective-permute-done.1
  7.8 0.1 maximum_bitcast_fusion
  7.9 0.6 copy.11
  8.6 0.0 copy-start
  8.6 0.9 copy-done
  9.5 58.8 %shard_map.59.x_ref = f32[4,8,64,1024]{3,2,1,0:T(8,128)} custom-call(f32[30,1024]{1,0:T(8,128)S(1)} %copy-done, f32[4,64,8,1024]{3,2,1,0:T(8,128)} %bitcast.13, f32[4,8,8,1024]{3,2,1,0:T(8,128)S(1)} %bitcast.12), custom_call_target="tpu_custom_call" | custom-call | tf_op jit(solution)/shard_map/pallas_call | solution.py:209
  68.2 189.6 %shard_map.60 = (f32[4,8,64,1024]{3,2,1,0:T(8,128)}, f32[4,8,8,1024]{3,2,1,0:T(8,128)S(1)}) custom-call(f32[4,8,64,1024]{3,2,1,0:T(8,128)} %shard_map.59.x_ref), custom_call_target="tpu_custom_call" | custom-call | tf_op jit(solution)/shard_map/pallas_call | solution.py:413
  257.9 0.0 copy-start.1
  257.9 0.0 copy-start.2
  257.9 11.6 %copy.10 = f32[4,64,8,1024]{3,2,1,0:T(8,128)} copy(f32[4,64,8,1024]{3,1,2,0:T(8,128)} %bitcast.15) | data formatting | bytes 16777216 | tf_op jit(solution)/shard_map/transpose | solution.py:519
  269.5 0.2 reduce_sum.18
  269.8 1.1 reshape.53
  270.9 0.2 reduce_sum.19
  271.1 0.1 reshape.54
  271.2 0.0 copy-done.1
  271.2 0.1 fusion.1
  271.3 0.6 scatter.4.x_ref
  272.0 9.8 %shard_map.61 = f32[8,128]{1,0:T(8,128)} custom-call(f32[8,128]{1,0:T(8,128)} %scatter.4.x_ref), custom_call_target="tpu_custom_call" | custom-call | tf_op jit(solution)/shard_map/pallas_call | solution.py:500
  281.8 0.0 copy-done.2
  281.8 1.3 slice_multiply_fusion
Async XLA Ops:
  1.9 4.4 %collective-permute-start = (f32[4,32,1024]{2,1,0:T(8,128)S(1)}, f32[4,32,1024]{2,1,0:T(8,128)S(1)}, u32[]{:S(2)}, u32[]{:S(2)}) collective-permute-start(f32[4,32,1024]{2,1,0:T(8,128)S(1)} %get-tuple-element.18), channel_id=1, source_target_pairs={{1,0},{3,2},{5,4},{7,6},{9,8},{11,10},{13,12},{15,14},{17,16},{19,... | collective-permute-start | bytes 1572872 | tf_op jit(solution)/shard_map/ppermute | solution.py:77
  3.2 4.6 %collective-permute-start.1 = (f32[4,32,1024]{2,1,0:T(8,128)S(1)}, f32[4,32,1024]{2,1,0:T(8,128)S(1)}, u32[]{:S(2)}, u32[]{:S(2)}) collective-permute-start(f32[4,32,1024]{2,1,0:T(8,128)S(1)} %get-tuple-element.19), channel_id=1, source_target_pairs={{0,1},{2,3},{4,5},{6,7},{8,9},{10,11},{12,13},{14,15},{16,17},{18,... | collective-permute-start | bytes 1572872 | tf_op jit(solution)/shard_map/ppermute | solution.py:77
  8.6 0.9 copy-start
  257.9 13.3 %copy-start.1 = (f32[64,10]{1,0:T(8,128)S(1)}, f32[64,10]{1,0:T(8,128)}, u32[]{:S(2)}) copy-start(f32[64,10]{1,0:T(8,128)} %constant.35.clone) | copy-start | bytes 7684
  257.9 23.9 %copy-start.2 = (f32[4,10]{1,0:T(4,128)S(1)}, f32[4,10]{1,0:T(4,128)}, u32[]{:S(2)}) copy-start(f32[4,10]{1,0:T(4,128)} %constant.40) | copy-start | bytes 484

commit v3 on v2

--- a/solution.py
+++ b/solution.py
@@ -107,13 +107,12 @@
     return table.astype(np.float32)
 
 
-def spatial_kernel(tab_ref, x_ref, halo_ref, o_ref, xin, buf, x_sem, h_sem):
+def spatial_frame(frame, frames, tab_ref, x_ref, halo_ref, o_ref, xin, buf, x_sem, h_sem):
     groups, width = buf.shape[1:]
     inner = groups - 2 * MARGIN
     row = lax.axis_index("row")
     at_top = row == 0
     at_bottom = row == lax.axis_size("row") - 1
-    frame = pl.program_id(0)
     slot = frame % 2
 
     def copies(f, slot):
@@ -130,7 +129,7 @@
         for copy in copies(frame, slot):
             copy.start()
 
-    @pl.when(frame + 1 < pl.num_programs(0))
+    @pl.when(frame + 1 < frames)
     def _():
         for copy in copies(frame + 1, 1 - slot):
             copy.start()
@@ -189,37 +188,10 @@
                 if low and level < SLEVELS - 1:
                     buf[p, :, lanes] = value
                 else:
-                    o_ref[0, p, :, lanes] = value[:inner]
+                    o_ref[frame, p, :, lanes] = value[:inner]
             return carry
 
         lax.fori_loop(0, width // 128, rows, 0)
-
-
-def spatial(footage):
-    frames, rows, width = footage.shape
-    edge = MARGIN * PERIOD
-    inner = rows // PERIOD
-    groups = inner + 2 * MARGIN
-    above = shifted(footage[:, -edge:], "row", 1)
-    below = shifted(footage[:, :edge], "row", -1)
-    halo = jnp.concatenate([below, above], axis=1)
-    halo = halo.reshape(frames, 2 * MARGIN, PERIOD, width).transpose(0, 2, 1, 3)
-    table = jnp.asarray(lane_table(width))
-    any_space = pl.BlockSpec(memory_space=pl.ANY)
-    return pl.pallas_call(
-        spatial_kernel,
-        grid=(frames,),
-        out_shape=jax.ShapeDtypeStruct((frames, PERIOD, inner, width), jnp.float32),
-        in_specs=[pl.BlockSpec(table.shape, lambda i: (0, 0)), any_space, any_space],
-        out_specs=pl.BlockSpec((1, PERIOD, inner, width), lambda i: (i, 0, 0, 0)),
-        scratch_shapes=[
-            pltpu.VMEM((2, PERIOD, groups, width), jnp.float32),
-            pltpu.VMEM((PERIOD, groups, width), jnp.float32),
-            pltpu.SemaphoreType.DMA((2, PERIOD)),
-            pltpu.SemaphoreType.DMA((2, PERIOD)),
-        ],
-        compiler_params=pltpu.CompilerParams(vmem_limit_bytes=50 * 2**20),
-    )(table, footage.reshape(frames, inner, PERIOD, width), halo)
 
 
 def outgoing(f):
@@ -260,10 +232,13 @@
     return out
 
 
-def exchange_kernel(x_ref, o_ref, sums_ref, held, from_before, from_after, to_before, to_after,
-                    f_send, f_recv, f_own, h_send, h_recv, r_send, r_recv, r_own):
-    frames, phases, inner, width = x_ref.shape
+def video_kernel(tab_ref, x_ref, halo_ref, o_ref, sums_ref, xin, buf, planes, mine, held,
+                 from_before, from_after, to_before, to_after, x_sem, e_sem,
+                 f_send, f_recv, f_own, h_send, h_recv, r_send, r_recv, r_own, m_own):
+    frames, phases, inner, width = planes.shape
     part = inner // GROUP
+    inside = [n for n in range(1, frames - 1, 2)]
+    moved = [n for n in range(frames) if n not in inside]
     me = lax.axis_index("frame")
     count = lax.axis_size("frame")
     member = me % GROUP
@@ -282,23 +257,23 @@
     def part_of(device):
         return pl.ds(pl.multiple_of((device % GROUP) * part, 8), part)
 
-    def frames_of(device):
-        return pl.ds((device % GROUP) * frames, frames)
-
-    def forward(c, k):
+    def spot(device, n):
+        return (device % GROUP) * frames + n
+
+    def forward(n, c, k):
         peer = peers[k]
         return pltpu.make_async_remote_copy(
-            src_ref=x_ref.at[:, c, part_of(peer), :],
-            dst_ref=held.at[frames_of(me), c],
-            send_sem=f_send.at[k, c],
-            recv_sem=f_recv.at[k, c],
+            src_ref=planes.at[n, c, part_of(peer), :],
+            dst_ref=held.at[spot(me, n), c],
+            send_sem=f_send.at[n, k, c],
+            recv_sem=f_recv.at[n, k, c],
             device_id={"frame": peer},
             device_id_type=MESH,
         )
 
-    def forward_own(c):
+    def forward_own(n, c):
         return pltpu.make_async_copy(
-            x_ref.at[:, c, part_of(me), :], held.at[frames_of(me), c], f_own.at[c]
+            planes.at[n, c, part_of(me), :], held.at[spot(me, n), c], f_own.at[n, c]
         )
 
     def halo(c, side):
@@ -311,37 +286,54 @@
             device_id_type=MESH,
         )
 
-    def back(c, k):
+    def back(i, c, k):
         peer = peers[k]
         return pltpu.make_async_remote_copy(
-            src_ref=held.at[frames_of(peer), c],
-            dst_ref=o_ref.at[:, c, part_of(me), :],
-            send_sem=r_send.at[k, c],
-            recv_sem=r_recv.at[k, c],
+            src_ref=held.at[spot(peer, moved[i]), c],
+            dst_ref=o_ref.at[moved[i], c, part_of(me), :],
+            send_sem=r_send.at[i, k, c],
+            recv_sem=r_recv.at[i, k, c],
             device_id={"frame": peer},
             device_id_type=MESH,
         )
 
-    def back_own(c):
+    def back_own(i, c):
         return pltpu.make_async_copy(
-            held.at[frames_of(me), c], o_ref.at[:, c, part_of(me), :], r_own.at[c]
-        )
-
-    def start_forward(c, carry):
-        for k in range(GROUP - 1):
-            forward(c, k).start()
-        forward_own(c).start()
-        return carry
-
-    lax.fori_loop(0, phases, start_forward, 0)
+            held.at[spot(me, moved[i]), c], o_ref.at[moved[i], c, part_of(me), :], r_own.at[i, c]
+        )
+
+    def keep(i, c):
+        return pltpu.make_async_copy(mine.at[i, c], o_ref.at[inside[i], c], m_own.at[i, c])
+
+    def one_frame(n, carry):
+        spatial_frame(n, frames, tab_ref, x_ref, halo_ref, planes, xin, buf, x_sem, e_sem)
+
+        def start_forward(c, carry):
+            for k in range(GROUP - 1):
+                forward(n, c, k).start()
+            forward_own(n, c).start()
+            return carry
+
+        return lax.fori_loop(0, phases, start_forward, carry)
+
+    lax.fori_loop(0, frames, one_frame, 0)
+
+    def inside_highs(c, carry):
+        for i, n in enumerate(inside):
+            mine[i, c] = planes[n, c] - 0.5 * (planes[n - 1, c] + planes[n + 1, c])
+            keep(i, c).start()
+        return carry
+
+    lax.fori_loop(0, phases, inside_highs, 0)
     total = GROUP * frames
     strip = 128
     strips = width // strip
 
     def send_halo(c):
-        for k in range(GROUP - 1):
-            forward(c, k).wait_recv()
-        forward_own(c).wait()
+        for n in range(frames):
+            for k in range(GROUP - 1):
+                forward(n, c, k).wait_recv()
+            forward_own(n, c).wait()
 
         def tile(i, carry):
             lanes = pl.ds(pl.multiple_of(i * strip, strip), strip)
@@ -367,7 +359,8 @@
             out = temporal(f, before, after, is_first, is_last)
             sums = [None] * (TLEVELS + 1)
             for n in range(total):
-                held[n, c, :, lanes] = out[n]
+                if n % frames in moved:
+                    held[n, c, :, lanes] = out[n]
                 t = level_of(n % 2**TLEVELS, TLEVELS) - 1
                 square = out[n] * out[n]
                 sums[t] = square if sums[t] is None else sums[t] + square
@@ -378,9 +371,10 @@
             return carry
 
         lax.fori_loop(0, strips, tile, 0)
-        for k in range(GROUP - 1):
-            back(c, k).start()
-        back_own(c).start()
+        for i in range(len(moved)):
+            for k in range(GROUP - 1):
+                back(i, c, k).start()
+            back_own(i, c).start()
 
     send_halo(0)
 
@@ -394,41 +388,64 @@
 
     def drain(c, carry):
         for k in range(GROUP - 1):
-            forward(c, k).wait_send()
-            back(c, k).wait()
+            for n in range(frames):
+                forward(n, c, k).wait_send()
+            for i in range(len(moved)):
+                back(i, c, k).wait()
         for side in range(2):
             halo(c, side).wait_send()
-        back_own(c).wait()
+        for i in range(len(moved)):
+            back_own(i, c).wait()
+        for i in range(len(inside)):
+            keep(i, c).wait()
         return carry
 
     lax.fori_loop(0, phases, drain, 0)
 
 
-def exchange(planes):
-    frames, phases, inner, width = planes.shape
+def transformed(footage):
+    frames, rows, width = footage.shape
+    edge = MARGIN * PERIOD
+    inner = rows // PERIOD
+    groups = inner + 2 * MARGIN
     part = inner // GROUP
+    above = shifted(footage[:, -edge:], "row", 1)
+    below = shifted(footage[:, :edge], "row", -1)
+    halo = jnp.concatenate([below, above], axis=1)
+    halo = halo.reshape(frames, 2 * MARGIN, PERIOD, width).transpose(0, 2, 1, 3)
+    table = jnp.asarray(lane_table(width))
     any_space = pl.BlockSpec(memory_space=pl.ANY)
-    halo_buffer = pltpu.VMEM((phases, TLEVELS, part, width), jnp.float32)
+    vmem = pl.BlockSpec(memory_space=pltpu.VMEM)
+    halo_buffer = pltpu.VMEM((PERIOD, TLEVELS, part, width), jnp.float32)
     dma = pltpu.SemaphoreType.DMA
+    kept = len(range(1, frames - 1, 2))
+    sent = frames - kept
     return pl.pallas_call(
-        exchange_kernel,
+        video_kernel,
         out_shape=(
-            jax.ShapeDtypeStruct(planes.shape, jnp.float32),
-            jax.ShapeDtypeStruct((TLEVELS + 1, phases, 8, width), jnp.float32),
+            jax.ShapeDtypeStruct((frames, PERIOD, inner, width), jnp.float32),
+            jax.ShapeDtypeStruct((TLEVELS + 1, PERIOD, 8, width), jnp.float32),
         ),
-        in_specs=[any_space],
-        out_specs=(any_space, pl.BlockSpec(memory_space=pltpu.VMEM)),
+        in_specs=[vmem, any_space, any_space],
+        out_specs=(any_space, vmem),
         scratch_shapes=[
-            pltpu.VMEM((GROUP * frames, phases, part, width), jnp.float32),
+            pltpu.VMEM((2, PERIOD, groups, width), jnp.float32),
+            pltpu.VMEM((PERIOD, groups, width), jnp.float32),
+            pltpu.VMEM((frames, PERIOD, inner, width), jnp.float32),
+            pltpu.VMEM((kept, PERIOD, inner, width), jnp.float32),
+            pltpu.VMEM((GROUP * frames, PERIOD, part, width), jnp.float32),
             halo_buffer, halo_buffer, halo_buffer, halo_buffer,
-            dma((GROUP - 1, phases)), dma((GROUP - 1, phases)), dma((phases,)),
-            dma((2, phases)), dma((2, phases)),
-            dma((GROUP - 1, phases)), dma((GROUP - 1, phases)), dma((phases,)),
+            dma((2, PERIOD)), dma((2, PERIOD)),
+            dma((frames, GROUP - 1, PERIOD)), dma((frames, GROUP - 1, PERIOD)),
+            dma((frames, PERIOD)),
+            dma((2, PERIOD)), dma((2, PERIOD)),
+            dma((sent, GROUP - 1, PERIOD)), dma((sent, GROUP - 1, PERIOD)),
+            dma((sent, PERIOD)), dma((kept, PERIOD)),
         ],
         compiler_params=pltpu.CompilerParams(
-            collective_id=0, has_side_effects=True, vmem_limit_bytes=50 * 2**20
+            collective_id=0, has_side_effects=True, vmem_limit_bytes=56 * 2**20
         ),
-    )(planes)
+    )(table, footage.reshape(frames, inner, PERIOD, width), halo)
 
 
 def total_kernel(x_ref, o_ref, inbox, send, recv):
@@ -514,8 +531,7 @@
 
 def shards(footage):
     frames, rows, width = footage.shape
-    planes = spatial(footage)
-    coeffs, sums = exchange(planes)
+    coeffs, sums = transformed(footage)
     coeffs = coeffs.transpose(0, 2, 1, 3).reshape(frames, rows, width)
     pattern = sums.sum(axis=2).reshape(TLEVELS + 1, PERIOD, width // PERIOD, PERIOD).sum(axis=2)
     pattern = pattern.reshape(TLEVELS + 1, PERIOD * PERIOD)

time: 283 us -> 222 us (0.78)
  Pallas kernels: 258 us -> 196 us
    pallas_call x2 -> x1, Pallas kernels: 248 us -> 187 us  [transformed(): pl.pallas_call(video_kernel, out_shape=(jax.ShapeDtypeStruct((frames, PER...]
where the time goes in v3:
time: 222 us; the launch traced here: 221 us
  Pallas kernels  196 us (88%)
  local copies, waits for them, and re-layouts  16.5 us (7%)
  starting transfers between devices  4.38 us (2%)
    pallas_call x1, Pallas kernels, transformed(): pl.pallas_call(video_kernel, out_shape=(jax.ShapeDtypeStruct((frames, PER...  187 us
    transpose x1, local copies, waits for them, and re-layouts, shards(): coeffs = coeffs.transpose(0, 2, 1, 3).reshape(frames, rows, width)  11.7 us
    pallas_call x1, Pallas kernels, total_over_devices(): pl.pallas_call(total_kernel, out_shape=jax.ShapeDtypeStruct((8, 128), jnp...  9.8 us
  transfers between devices with their start and end apart: 2, of which 1 were waited for; matrix products, arithmetic and copies ran while one was open for 0% of the time, Pallas kernels for 0%

profile of v3, /device:TPU:0, one launch (start us, length us, event | category | flops | bytes accessed | tf_op | source)
XLA Modules:
  0.0 221.3 jit_solution(2367441440197192198)
XLA Ops:
  0.6 1.3 fusion
  1.9 1.3 collective-permute-start
  3.2 3.1 %collective-permute-start.1 = (f32[4,32,1024]{2,1,0:T(8,128)S(1)}, f32[4,32,1024]{2,1,0:T(8,128)S(1)}, u32[]{:S(2)}, u32[]{:S(2)}) collective-permute-start(f32[4,32,1024]{2,1,0:T(8,128)S(1)} %get-tuple-element.19), channel_id=1, source_target_pairs={{0,1},{2,3},{4,5},{6,7},{8,9},{10,11},{12,13},{14,15},{16,17},{18,... | collective-permute-start | bytes 1572872 | tf_op jit(solution)/shard_map/ppermute | solution.py:77
  6.3 0.0 collective-permute-done
  6.4 1.5 collective-permute-done.1
  7.8 0.1 maximum_bitcast_fusion
  7.9 1.6 copy.11
  9.5 186.5 %shard_map.59 = (f32[4,8,64,1024]{3,2,1,0:T(8,128)}, f32[4,8,8,1024]{3,2,1,0:T(8,128)}) custom-call(f32[30,1024]{1,0:T(8,128)} %constant.34.clone.tab_ref, f32[4,64,8,1024]{3,2,1,0:T(8,128)} %bitcast.12, f32[4,8,8,1024]{3,2,1,0:T(8,128)} %bitcast.15), custom_call_target="tpu_custom_call" | custom-call | tf_op jit(solution)/shard_map/pallas_call | solution.py:423
  196.1 0.0 copy-start
  196.1 0.0 copy-start.1
  196.1 0.0 copy-start.2
  196.1 11.7 %copy.10 = f32[4,64,8,1024]{3,2,1,0:T(8,128)} copy(f32[4,64,8,1024]{3,1,2,0:T(8,128)} %bitcast.14) | data formatting | bytes 16777216 | tf_op jit(solution)/shard_map/transpose | solution.py:535
  207.8 0.0 copy-done
  207.8 0.2 reduce_sum.18
  208.1 1.1 reshape.53
  209.2 0.2 reduce_sum.19
  209.4 0.1 reshape.54
  209.5 0.0 copy-done.1
  209.5 0.1 fusion.1
  209.6 0.6 scatter.4.x_ref
  210.2 9.8 %shard_map.60 = f32[8,128]{1,0:T(8,128)} custom-call(f32[8,128]{1,0:T(8,128)} %scatter.4.x_ref), custom_call_target="tpu_custom_call" | custom-call | tf_op jit(solution)/shard_map/pallas_call | solution.py:517
  220.0 0.0 copy-done.2
  220.1 1.3 slice_multiply_fusion
Async XLA Ops:
  1.9 4.4 %collective-permute-start = (f32[4,32,1024]{2,1,0:T(8,128)S(1)}, f32[4,32,1024]{2,1,0:T(8,128)S(1)}, u32[]{:S(2)}, u32[]{:S(2)}) collective-permute-start(f32[4,32,1024]{2,1,0:T(8,128)S(1)} %get-tuple-element.18), channel_id=1, source_target_pairs={{1,0},{3,2},{5,4},{7,6},{9,8},{11,10},{13,12},{15,14},{17,16},{19,... | collective-permute-start | bytes 1572872 | tf_op jit(solution)/shard_map/ppermute | solution.py:77
  3.2 4.6 %collective-permute-start.1 = (f32[4,32,1024]{2,1,0:T(8,128)S(1)}, f32[4,32,1024]{2,1,0:T(8,128)S(1)}, u32[]{:S(2)}, u32[]{:S(2)}) collective-permute-start(f32[4,32,1024]{2,1,0:T(8,128)S(1)} %get-tuple-element.19), channel_id=1, source_target_pairs={{0,1},{2,3},{4,5},{6,7},{8,9},{10,11},{12,13},{14,15},{16,17},{18,... | collective-permute-start | bytes 1572872 | tf_op jit(solution)/shard_map/ppermute | solution.py:77
  196.1 11.8 %copy-start = (f32[4,8,8,1024]{3,2,1,0:T(8,128)S(1)}, f32[4,8,8,1024]{3,2,1,0:T(8,128)}, u32[]{:S(2)}) copy-start(f32[4,8,8,1024]{3,2,1,0:T(8,128)} %get-tuple-element.17) | copy-start | bytes 3145732
  196.1 13.4 %copy-start.1 = (f32[64,10]{1,0:T(8,128)S(1)}, f32[64,10]{1,0:T(8,128)}, u32[]{:S(2)}) copy-start(f32[64,10]{1,0:T(8,128)} %constant.35.clone) | copy-start | bytes 7684
  196.1 24.0 %copy-start.2 = (f32[4,10]{1,0:T(4,128)S(1)}, f32[4,10]{1,0:T(4,128)}, u32[]{:S(2)}) copy-start(f32[4,10]{1,0:T(4,128)} %constant.40) | copy-start | bytes 484
